TPU v7x, 128 devices: a whole 4x4x4 slice. The times are simulated.
128 devices in a mesh: graph: 32 (over z, x, core), batch: 4 (over y).
Axes of the slice: x: 4, y: 4, z: 4, core: 2. Of those that a mesh axis runs over, the one named last changes fastest.
Arguments:
- node_latent: bfloat16 [4, 4096, 512], P('batch', 'graph'), may hold values from -6 to 6
- edge_latent: bfloat16 [4, 32768, 512], P('batch', 'graph'), may hold values from -6 to 6
- node_cotangent: bfloat16 [4, 4096, 512], P('batch', 'graph'), may hold values from -6 to 6
- edge_w_in: bfloat16 [2, 1536, 512], replicated, may hold values from -0.15625 to 0.15625
- edge_w_out: bfloat16 [2, 512, 512], replicated, may hold values from -0.25 to 0.25
- node_w_in: bfloat16 [2, 1024, 512], replicated, may hold values from -0.1875 to 0.1875
- node_w_out: bfloat16 [2, 512, 512], replicated, may hold values from -0.25 to 0.25
- edge_gain: float32 [2, 512], replicated, may hold values from 0.25 to 1.75
- node_gain: float32 [2, 512], replicated, may hold values from 0.25 to 1.75
- edge_slot: int32 [32768], P('graph'), may hold values from 0 to 1151, as said below
- edge_receiver: int32 [32768], P('graph'), may hold values from 0 to 127
- send_list: int32 [1024, 32], P('graph'), may hold values from 0 to 127, as said below
- edge_count: int32 [32], P('graph'), may hold values from 256 to 1024, as said below
Outputs:
- node_out: float32 [4, 4096, 512], P('batch', 'graph')
- node_grad: float32 [4, 4096, 512], P('batch', 'graph')
- grad_edge_in: float32 [2, 1536, 512], P(None, ('graph', 'batch'))
- grad_edge_out: float32 [2, 512, 512], P(None, ('graph', 'batch'))
- grad_node_in: float32 [2, 1024, 512], P(None, ('graph', 'batch'))
- grad_node_out: float32 [2, 512, 512], P(None, ('graph', 'batch'))
- grad_edge_gain: float32 [2, 512], P(None, ('graph', 'batch'))
- grad_node_gain: float32 [2, 512], P(None, ('graph', 'batch'))
Inputs may be any that keep to these rules, and one draw needn't show every extreme that they name: `edge_slot`: for edge j of partition p = j // 1024: a slot below 128 names a node of partition p; a slot s of 128 or more names row (s - 128) % 32 of the list that partition q = (s - 128) // 32 keeps for partition p, and q differs from p cyclically by 1 to 2 steps or by exactly 32 // 2 steps. `edge_receiver`: the receiving node is a node of the edge's own partition. `send_list`: row q * 32 + p holds 32 distinct node numbers within partition q, the nodes whose latents partition p may read. `edge_count`: edge slots at or above a partition's count carry no edge.
All inputs are finite; a program needn't handle non-finite values.
Results may differ from a plain program's by a relative error of at most 0.035.
Values may be sent and summed in bfloat16 or wider, within the bound.
A program may use at most 128 MiB of HBM per device.

v0:
```python
import types

import jax
import jax.numpy as jnp
from jax import lax
from jax.experimental import pallas as pl
from jax.experimental.pallas import tpu as pltpu
from jax.sharding import PartitionSpec as P

HOPS = 2
EPSILON = 1e-05
BF = jnp.bfloat16
F32 = jnp.float32
D = 512
NODES = 128
EDGES = 1024
PEER = 32
GROUP = 32
SAMPLES = 4
VMEM_LIMIT = 62 * 1024 * 1024
OFFSETS = tuple(o for o in range(-HOPS, HOPS + 1) if o != 0) + (GROUP // 2,)
HALO = len(OFFSETS) * PEER
RECV_AT = NODES
HALO_AT = 2 * NODES
SUMS_AT = 2 * NODES
FIRST, FORE, BACK = 1024, 1024, 512
FORE_UNROLL, BACK_UNROLL = 1, 1
MESH = pl.DeviceIdType.MESH
STREAM_TILES = (((16, 512),) * 3, ((8, 384), (8, 384), (24, 128)))
PART_ORDER = ((1, 2, 0), (2, 0, 1), (0, 1, 2))
AXES = ("graph", "batch")
scope = jax.named_scope


def dot(a, b):
    return jnp.dot(a, b, preferred_element_type=F32)


def dot_tb(a, b):
    return lax.dot_general(a, b, (((1,), (1,)), ((), ())), preferred_element_type=F32)


def dot_ta(a, b):
    return lax.dot_general(a, b, (((0,), (0,)), ((), ())), preferred_element_type=F32)


def place_id(graph, batch):
    return dict(zip(AXES, (graph, batch)))


def wrap(value, size):
    return lax.rem(value + 2 * size, size)


def iota(shape, dim):
    return lax.broadcasted_iota(jnp.int32, shape, dim)


def half_shape(part):
    first, second, _ = PART_ORDER[part]
    shape = [4, 4, 4]
    shape[second] = 2
    del shape[first]
    return tuple(shape)


NL, EWI, EL, EWO, NWI, NWO, COT = 0, (1, 6), 2, (3, 7), (4, 8), (5, 9), 10


def scratch_spec():
    vm = pltpu.VMEM

    def two(shape, dtype):
        return [vm(shape, dtype), vm(shape, dtype)]

    def parts(shape):
        keys = [(stream, part) for stream in range(2) for part in range(3)]
        return {key: vm(shape(key[1]) + STREAM_TILES[key[0]][key[1]], BF) for key in keys}

    return dict(
        nl=vm((NODES, D), BF),
        el=vm((EDGES, D), BF),
        ewi=vm((2, 3 * D, D), BF),
        ewo=vm((2, D, D), BF),
        nwi=vm((2, 2 * D, D), BF),
        nwo=vm((2, D, D), BF),
        cot=vm((NODES, D), BF),
        cnt=pltpu.SMEM((1,), jnp.int32),
        SR=vm((EDGES, 512), BF),
        SRT=vm((512, EDGES), BF),
        LT=vm((NODES, HALO), BF),
        PS=vm((512, D), BF),
        PRE=vm((EDGES, D), F32),
        EB1=vm((EDGES, D), BF),
        VB1=vm((NODES, D), BF),
        V1=vm((NODES, D), F32),
        N=two((EDGES, D), BF),
        DA=two((EDGES, D), BF),
        H=two((EDGES, D), BF),
        INV=two((EDGES, 1), F32),
        NN=two((NODES, D), F32),
        NDA=two((NODES, D), F32),
        NH=two((NODES, D), BF),
        NINV=two((NODES, 1), F32),
        AGG=two((NODES, D), BF),
        HS=two((HALO, D), BF),
        HR=two((HALO, D), BF),
        BS=two((HALO, D), BF),
        BR=two((HALO, D), BF),
        G=parts(lambda part: (4, 4, 2, 4)),
        RC=parts(lambda part: (4, 4, 4)),
        RA=parts(lambda part: (6,) + half_shape(part)),
        CA=parts(lambda part: (2,) + half_shape(part)),
        AB=parts(lambda part: (4, 4)),
        RB=parts(lambda part: (3, 4)),
        AD=parts(lambda part: (4,)),
        RD=parts(lambda part: (3,)),
        GZ=vm((EDGES, D), BF),
        GA=vm((EDGES, D), BF),
        GE=vm((EDGES, D), F32),
        GSR=vm((HALO_AT, D), F32),
        GV=vm((NODES, D), F32),
        GACC=vm((8, D), F32),
        WE=vm((3 * D, D), F32),
        WEO=vm((D, D), F32),
        WN=vm((2 * D, D), F32),
        WNO=vm((D, D), F32),
        load=pltpu.SemaphoreType.DMA((12,)),
        halo_send=pltpu.SemaphoreType.DMA((2, 2, 5)),
        halo_recv=pltpu.SemaphoreType.DMA((2, 2, 5)),
        rs_send=pltpu.SemaphoreType.DMA((2, 3, 13)),
        rs_recv=pltpu.SemaphoreType.DMA((2, 3, 13)),
    )


def flat_scratch():
    return jax.tree.flatten(scratch_spec())


def kernel(*refs):
    far, (eg, ng, slot, rcv, slist), (out,) = refs[:8], refs[8:13], refs[13:14]
    r = types.SimpleNamespace(**jax.tree.unflatten(flat_scratch()[1], refs[14:]))
    g = lax.axis_index(AXES[0])
    y = lax.axis_index(AXES[1])
    core = lax.rem(g, 2)
    x = lax.rem(g // 2, 4)
    z = g // 8
    place = (z, x, y)

    def peer(axis, step):
        zz = wrap(z + step, 4) if axis == 0 else z
        xx = wrap(x + step, 4) if axis == 1 else x
        yy = wrap(y + step, 4) if axis == 2 else y
        return place_id((zz * 4 + xx) * 2 + core, yy)

    def graph_peer(offset):
        return place_id(wrap(g + offset, GROUP), y)

    other_core = place_id(g + 1 - 2 * core, y)

    barrier = pltpu.get_barrier_semaphore()
    greeted = 0
    for offset in OFFSETS:
        pl.semaphore_signal(barrier, inc=1, device_id=graph_peer(offset), device_id_type=MESH)
        pl.semaphore_signal(barrier, inc=1, device_id=graph_peer(-offset), device_id_type=MESH)
        greeted += 2
    for axis in range(3):
        for step in (1, 2, 3):
            pl.semaphore_signal(barrier, inc=1, device_id=peer(axis, step), device_id_type=MESH)
            greeted += 1
    pl.semaphore_signal(barrier, inc=1, device_id=other_core, device_id_type=MESH)
    greeted += 1

    nl, el, ewi, ewo, nwi, nwo, cot, cnt = far
    pairs = [(nl, r.nl), (ewi, r.ewi, 0), (el, r.el), (ewo, r.ewo, 0), (nwi, r.nwi, 0), (nwo, r.nwo, 0)]
    pairs += [(ewi, r.ewi, 1), (ewo, r.ewo, 1), (nwi, r.nwi, 1), (nwo, r.nwo, 1), (cot, r.cot), (cnt, r.cnt)]

    def load(number):
        src, dst, *layer = pairs[number]
        if layer:
            src, dst = src.at[layer[0]], dst.at[layer[0]]
        return pltpu.make_async_copy(src, dst, r.load.at[number])

    for number in (11,) + tuple(range(11)):
        load(number).start()

    listed = jnp.concatenate(
        [slist[pl.ds(wrap(g - offset, GROUP), 1), :] for offset in OFFSETS], axis=1
    ).astype(F32)
    node_ids = iota((NODES, HALO), 0).astype(F32)
    r.LT[...] = jnp.where(node_ids == listed, 1.0, 0.0).astype(BF)

    def halo_copies(layer, way):
        src, dst = ((r.HS, r.HR), (r.BS, r.BR))[way]
        src, dst = src[layer], dst[layer]
        copies = []
        for b in reversed(range(len(OFFSETS))):
            offset = OFFSETS[b]
            rows = pl.ds(b * PEER, PEER)
            copies.append(
                pltpu.make_async_remote_copy(
                    src_ref=src.at[rows],
                    dst_ref=dst.at[rows],
                    send_sem=r.halo_send.at[layer, way, b],
                    recv_sem=r.halo_recv.at[layer, way, b],
                    device_id=graph_peer(-offset if way == 0 else offset),
                    device_id_type=MESH,
                )
            )
        return copies

    def vb(layer):
        return r.nl if layer == 0 else r.VB1

    def eb(layer):
        return r.el if layer == 0 else r.EB1

    def one_hots():
        load(11).wait()
        s = slot[...]
        within = s - NODES
        source = within // PEER
        distance = wrap(source - g, GROUP)
        block = jnp.zeros_like(s)
        for b, offset in enumerate(OFFSETS):
            block = jnp.where(distance == offset % GROUP, b, block)
        position = jnp.where(s < NODES, s, HALO_AT + block * PEER + (within - source * PEER))
        edge = iota((8, 128), 0) * 128 + iota((8, 128), 1)
        receiver = jnp.where(edge < r.cnt[0], rcv[...] + RECV_AT, -1)
        position = position.astype(F32)
        receiver = receiver.astype(F32)
        row_ids = iota((512, 128), 0).astype(F32)
        lane_ids = iota((128, 512), 1).astype(F32)
        for i in range(8):
            prow = position[i : i + 1, :]
            rrow = receiver[i : i + 1, :]
            at = slice(i * 128, (i + 1) * 128)
            for j in range(4):
                rows = slice(j * 128, (j + 1) * 128)
                row = rrow if j == 1 else prow
                r.SRT[rows, at] = jnp.where(row_ids[rows] == row, 1.0, 0.0).astype(BF)
            pcol = jnp.broadcast_to(prow, (128, 128)).T
            rcol = jnp.broadcast_to(rrow, (128, 128)).T
            for j in range(4):
                col = rcol if j == 1 else pcol
                lanes = slice(j * 128, (j + 1) * 128)
                r.SR[at, lanes] = jnp.where(lane_ids[:, lanes] == col, 1.0, 0.0).astype(BF)

    def norm(projected):
        centre = projected - jnp.mean(projected, axis=-1, keepdims=True)
        inv_std = lax.rsqrt(jnp.mean(centre * centre, axis=-1, keepdims=True) + EPSILON)
        return centre * inv_std, inv_std

    def swish(pre_act):
        sigma = 0.5 * jnp.tanh(0.5 * pre_act) + 0.5
        hidden = pre_act * sigma
        return hidden, sigma + hidden * (1.0 - sigma)

    def tile_at(t, rows):
        return pl.ds(pl.multiple_of(t * rows, rows), rows)

    def forward(layer):
        w = r.ewi.at[layer]
        wo = r.ewo.at[layer]
        nw = r.nwi.at[layer]
        nwo = r.nwo.at[layer]
        gain = eg[layer : layer + 1, :]
        ps = r.PS
        with scope("f_send"):
            if layer == 0:
                load(NL).wait()
            r.HS[layer][...] = dot_ta(r.LT[...], vb(layer)[...]).astype(BF)
            copies = halo_copies(layer, 0)
            if layer == 0:
                pl.semaphore_wait(barrier, greeted)
            for copy in copies:
                copy.start()
        with scope("f_first"):
            if layer == 0:
                one_hots()
            node = vb(layer)[...]
            load(EWI[layer]).wait()
            ps[0:NODES] = dot(node, w[D : 2 * D]).astype(BF)
            ps[RECV_AT:HALO_AT] = dot(node, w[2 * D :]).astype(BF)
            if layer == 0:
                ps[HALO_AT + HALO :] = jnp.zeros((512 - HALO_AT - HALO, D), BF)
                load(EL).wait()

            def first(t, carry):
                at = tile_at(t, FIRST)
                r.PRE[at] = dot(eb(layer)[at], w[0:D]) + dot(r.SR[at, 0:HALO_AT], ps[0:HALO_AT])
                return carry

            lax.fori_loop(0, EDGES // FIRST, first, 0)
        with scope("f_halo_wait"):
            load(EWO[layer]).wait()
            load(NWI[layer]).wait()
            load(NWO[layer]).wait()
            for copy in copies:
                copy.wait()
        with scope("f_edges"):
            ps[HALO_AT : HALO_AT + HALO] = dot(r.HR[layer][...], w[D : 2 * D]).astype(BF)

            def edges(t, carry):
                at = tile_at(t, FORE)
                pre_act = r.PRE[at] + dot(r.SR[at, HALO_AT:], ps[HALO_AT:])
                hidden, slope = swish(pre_act)
                hidden = hidden.astype(BF)
                r.H[layer][at] = hidden
                r.DA[layer][at] = slope.astype(BF)
                normed, inv_std = norm(dot(hidden, wo[...]))
                r.INV[layer][at] = inv_std
                r.N[layer][at] = normed.astype(BF)
                if layer == 0:
                    r.EB1[at] = (r.el[at].astype(F32) + normed * gain).astype(BF)
                return carry

            lax.fori_loop(0, EDGES // FORE, edges, 0, unroll=FORE_UNROLL)
        with scope("f_node"):
            agg = (dot(r.SRT[RECV_AT:HALO_AT], r.N[layer][...]) * gain).astype(BF)
            r.AGG[layer][...] = agg
            pre_act = dot(node, nw[0:D]) + dot(agg, nw[D:])
            hidden, slope = swish(pre_act)
            hidden = hidden.astype(BF)
            r.NH[layer][...] = hidden
            r.NDA[layer][...] = slope
            normed, inv_std = norm(dot(hidden, nwo[...]))
            r.NN[layer][...] = normed
            r.NINV[layer][...] = inv_std
            update = normed * ng[layer : layer + 1, :]
            if layer == 0:
                state = r.nl[...].astype(F32) + update
                r.V1[...] = state
                r.VB1[...] = state.astype(BF)
            else:
                out[0:NODES] = r.V1[...] + update

    def norm_back(grad, normed, inv_std):
        return inv_std * (
            grad
            - jnp.mean(grad, axis=-1, keepdims=True)
            - normed * jnp.mean(grad * normed, axis=-1, keepdims=True)
        )

    def fold_rows(a):
        return jnp.sum(a.reshape(a.shape[0] // 8, 8, a.shape[1]), axis=0)

    def backward_nodes(layer):
        nw = r.nwi.at[layer]
        node = vb(layer)[...]
        with scope("b_node"):
            grad = r.GV[...]
            normed = r.NN[layer][...]
            gain_sum = jnp.sum(grad * normed, axis=0, keepdims=True)
            gz = norm_back(grad * ng[layer : layer + 1, :], normed, r.NINV[layer][...]).astype(BF)
            ga = (dot_tb(gz, r.nwo[layer]) * r.NDA[layer][...]).astype(BF)
            grad_agg = dot_tb(ga, nw[D:]).astype(BF)
            r.GV[...] = grad + dot_tb(ga, nw[0:D])
            r.GACC[...] = jnp.zeros((8, D), F32)

        def weights():
            with scope("b_dwn"):
                r.WN[0:D] = dot_ta(node, ga)
                r.WN[D:] = dot_ta(r.AGG[layer][...], ga)
                r.WNO[...] = dot_ta(r.NH[layer][...], gz)

        return grad_agg, gain_sum, weights

    def backward_edges(layer, grad_agg, begin, end):
        w = r.ewi.at[layer]
        wo = r.ewo.at[layer]
        gain = eg[layer : layer + 1, :]

        def edges(t, carry):
            at = tile_at(t, BACK)
            gm = dot(r.SR[at, RECV_AT:HALO_AT], grad_agg)
            if layer == 0:
                gm = gm + r.GE[at]
            en = r.N[layer][at].astype(F32)
            r.GACC[...] += fold_rows(gm * en)
            ez = norm_back(gm * gain, en, r.INV[layer][at]).astype(BF)
            r.GZ[at] = ez
            ea = (dot_tb(ez, wo[...]) * r.DA[layer][at].astype(F32)).astype(BF)
            r.GA[at] = ea
            if layer == 1:
                r.GE[at] = dot_tb(ea, w[0:D])
            return carry

        with scope("b_edges"):
            lax.fori_loop(begin, end, edges, 0, unroll=BACK_UNROLL)

    def return_halo(layer):
        with scope("b_gsr"):
            sums = dot(r.SRT[...], r.GA[...])
            r.GSR[...] = sums[0:HALO_AT]
            r.BS[layer][...] = sums[HALO_AT : HALO_AT + HALO].astype(BF)
            copies = halo_copies(layer, 1)
            for copy in copies:
                copy.start()
        return copies

    def edge_weights(layer):
        node = vb(layer)[...]
        with scope("b_dwe"):
            r.WE[0:D] = dot_ta(eb(layer)[...], r.GA[...])
            r.WEO[...] = dot_ta(r.H[layer][...], r.GZ[...])
            to_sender = r.GSR[0:NODES].astype(BF)
            to_receiver = r.GSR[RECV_AT:HALO_AT].astype(BF)
            r.WE[D : 2 * D] = dot_ta(node, to_sender) + dot_ta(r.HR[layer][...], r.BS[layer][...])
            r.WE[2 * D :] = dot_ta(node, to_receiver)
        return jnp.sum(r.GACC[...], axis=0, keepdims=True)

    def take_halo(layer, copies):
        w = r.ewi.at[layer]
        with scope("b_halo_wait"):
            for copy in copies:
                copy.wait()
        with scope("b_tail"):
            to_sender = (r.GSR[0:NODES] + dot(r.LT[...], r.BR[layer][...])).astype(BF)
            to_receiver = r.GSR[RECV_AT:HALO_AT].astype(BF)
            total = r.GV[...] + dot_tb(to_sender, w[D : 2 * D]) + dot_tb(to_receiver, w[2 * D :])
            r.GV[...] = total
        return total

    low = iota((8, D), 0) < 4

    def each_pair(make):
        def slab(zz, carry):
            for xx in range(4):
                for cc in range(2):
                    for yy in range(2):
                        make((zz, xx, cc), 2 * yy, (zz, (xx * 2 + cc) * 2 + yy))
            return carry

        lax.fori_loop(0, 4, slab, 0)

    def pair_rows(ref, k, start, size):
        zz, inner = k
        return ref[pl.ds(pl.multiple_of(zz * 16 * size, 8) + inner * size + start, 8), :]

    def edge_slots(k):
        e0, e1, e2 = (pair_rows(r.WE, k, 8 * i, 24) for i in range(3))
        out = pltpu.roll(pair_rows(r.WEO, k, 0, 8), 4, 0)
        return (e0, jnp.where(low, e1, out)), (e2, jnp.where(low, out, e1))

    def assemble_edges(layer, gain_sum):
        def pair(where, yy, k):
            for odd, (g0, g1) in enumerate(edge_slots(k)):
                at = where + (yy + odd,)
                if layer == 1:
                    r.G[0, 0][at] = jnp.concatenate([g0, g1], axis=0).astype(BF)
                else:
                    r.G[1, 0][at] = g0[:, 0:384].astype(BF)
                    r.G[1, 1][at] = g1[:, 0:384].astype(BF)
                    r.G[1, 2][at] = jnp.concatenate([g0[:, 384:], g1[:, 384:], gains], axis=0).astype(BF)

        if layer == 0:
            lanes = [gain_sum[:, 128 * i : 128 * (i + 1)] for i in range(4)]
            gains = jnp.zeros((8, 128), F32)
            for i in range(4):
                gains = jnp.where(iota((8, 128), 0) == i, lanes[i], gains)
        with scope("asm_edges"):
            each_pair(pair)

    def assemble_nodes(layer, *gain_sums):
        row = iota((8, D), 0) % 4
        gains = jnp.zeros((8, D), F32)
        for i, gain_sum in enumerate(gain_sums):
            gains = jnp.where(row == i, gain_sum, gains)
        target = r.G[0, 1] if layer == 1 else r.G[0, 2]

        def pair(where, yy, k):
            n0, n1 = (pair_rows(r.WN, k, 8 * i, 16) for i in range(2))
            last = pair_rows(r.WNO, k, 0, 8)
            even = jnp.concatenate([n0, jnp.where(low, last, gains)], axis=0)
            odd = jnp.concatenate([n1, jnp.where(low, gains, last)], axis=0)
            target[where + (yy,)] = even.astype(BF)
            target[where + (yy + 1,)] = odd.astype(BF)

        with scope("asm_nodes"):
            each_pair(pair)

    def rs_copy(key, number, src, dst, device):
        return pltpu.make_async_remote_copy(
            src_ref=src,
            dst_ref=dst,
            send_sem=r.rs_send.at[key[0], key[1], number],
            recv_sem=r.rs_recv.at[key[0], key[1], number],
            device_id=device,
            device_id_type=MESH,
        )

    def cores(key):
        return rs_copy(key, 0, r.G[key].at[:, :, 1 - core], r.RC[key], other_core)

    def axes(key):
        first, second, third = PART_ORDER[key[1]]
        return first, second, third, second - (1 if first < second else 0)

    def cut(key, first_at, half):
        first, second, _, _ = axes(key)
        index = [slice(None)] * 3
        index[first] = first_at
        index[second] = pl.ds(2 * half, 2)
        return tuple(index)

    def ring(key, slot):
        axis = axes(key)[0]
        me = place[axis]
        way, kind = slot // 3, slot % 3
        sign = 1 - 2 * way
        if kind == 0:
            src = r.RC[key].at[cut(key, wrap(me + 2, 4), 1 - way)]
        elif kind == 1:
            src = r.RC[key].at[cut(key, wrap(me + sign, 4), way)]
        else:
            src = r.CA[key].at[way]
        return rs_copy(key, 1 + slot, src, r.RA[key].at[slot], peer(axis, sign))

    def second_copies(key):
        _, axis, _, at = axes(key)
        copies = []
        for step in (2, 1, 3):
            src = r.AB[key].at[(slice(None),) * at + (wrap(place[axis] + step, 4),)]
            copies.append(rs_copy(key, 6 + step, src, r.RB[key].at[step - 1], peer(axis, step)))
        return copies

    def third_copies(key):
        axis = axes(key)[2]
        copies = []
        for step in (2, 1, 3):
            src = r.AD[key].at[wrap(place[axis] + step, 4)]
            copies.append(rs_copy(key, 9 + step, src, r.RD[key].at[step - 1], peer(axis, step)))
        return copies

    def rs_cores(key):
        cores(key).start()

    def rs_ring(key):
        with scope("rs_ring"):
            cores(key).wait()
            mine, both = r.G[key], r.RC[key]

            def add(i, carry):
                both[i] = both[i] + mine[i, :, core]
                return carry

            lax.fori_loop(0, 4, add, 0)
            for slot in (0, 3, 1, 4):
                ring(key, slot).start()

    def rs_sums(key):
        with scope("rs_sums"):
            me = place[axes(key)[0]]
            for way, sign in ((0, 1), (1, -1)):
                ring(key, 3 * way).wait()
                own = r.RC[key][cut(key, wrap(me + sign, 4), 1 - way)]
                r.CA[key][way] = own + r.RA[key][3 * way]
                ring(key, 3 * way + 2).start()

    def rs_second(key):
        with scope("rs_second"):
            first, axis, _, at = axes(key)
            for slot in (1, 4, 2, 5):
                ring(key, slot).wait()
            got = r.RA[key]
            for half in range(2):
                near, summed = (1, 5) if half == 0 else (4, 2)
                total = r.RC[key][cut(key, place[first], half)].astype(F32)
                total = total + got[near].astype(F32) + got[summed].astype(F32)
                index = (slice(None),) * at + (slice(2 * half, 2 * half + 2),)
                r.AB[key][index] = total.astype(BF)
            for copy in second_copies(key):
                copy.start()

    def rs_third(key):
        with scope("rs_third"):
            _, axis, _, at = axes(key)
            for copy in second_copies(key):
                copy.wait()
            total = r.AB[key][(slice(None),) * at + (place[axis],)].astype(F32)
            for i in range(3):
                total = total + r.RB[key][i].astype(F32)
            r.AD[key][...] = total.astype(BF)
            for copy in third_copies(key):
                copy.start()

    def rs_finish(key):
        with scope("rs_finish"):
            for copy in third_copies(key):
                copy.wait()
            total = r.AD[key][place[axes(key)[2]]].astype(F32)
            for i in range(3):
                total = total + r.RD[key][i].astype(F32)
            stream, part = key
            if stream == 0:
                out[SUMS_AT + 16 * part : SUMS_AT + 16 * part + 16] = total
            elif part < 2:
                out[SUMS_AT + 48 + 8 * part : SUMS_AT + 56 + 8 * part, 0:384] = total
            else:
                for i in range(2):
                    out[SUMS_AT + 48 + 8 * i : SUMS_AT + 56 + 8 * i, 384:] = total[8 * i : 8 * i + 8]
                out[SUMS_AT + 64 :, 0:128] = total[16:24]

    early = ((0, 0), (0, 1), (0, 2))
    late = ((1, 0), (1, 1), (1, 2))

    def each(call, keys):
        for key in keys:
            call(key)

    forward(0)
    forward(1)
    load(COT).wait()
    r.GV[...] = r.cot[...].astype(F32)
    count = EDGES // BACK

    grad_agg, node_gain, node_weights = backward_nodes(1)
    backward_edges(1, grad_agg, 0, count)
    copies = return_halo(1)
    edge_gain = edge_weights(1)
    assemble_edges(1, None)
    rs_cores((0, 0))
    node_weights()
    assemble_nodes(1, edge_gain, node_gain)
    rs_cores((0, 1))
    take_halo(1, copies)
    rs_ring((0, 0))

    grad_agg, node_gain, node_weights = backward_nodes(0)
    node_weights()
    assemble_nodes(0, node_gain)
    rs_cores((0, 2))
    rs_ring((0, 1))
    backward_edges(0, grad_agg, 0, count)
    rs_ring((0, 2))
    copies = return_halo(0)
    rs_sums((0, 0))
    edge_gain = edge_weights(0)
    rs_sums((0, 1))
    assemble_edges(0, edge_gain)
    each(rs_cores, late)
    rs_sums((0, 2))
    each(rs_ring, late)
    out[NODES : 2 * NODES] = take_halo(0, copies)
    rs_second((0, 0))
    each(rs_sums, late)
    rs_second((0, 1))
    rs_second((0, 2))
    rs_third((0, 0))
    each(rs_second, late)
    rs_third((0, 1))
    rs_third((0, 2))
    each(rs_third, late)
    each(rs_finish, early)
    each(rs_finish, late)


def finish_kernel(sums, o_node, o_grad, o_ei, o_eo, o_ni, o_no, o_eg, o_ng):
    y = lax.axis_index(AXES[1])
    column = (lax.axis_index(AXES[0]) * SAMPLES + y) * 4
    is_even = lax.rem(y, 2) == 0
    o_node[...] = sums[0:NODES]
    o_grad[...] = sums[NODES : 2 * NODES]

    def edge_rows(layer, g0, g1):
        even = jnp.concatenate([g0, g1[0:4]], axis=0)
        odd = jnp.concatenate([g1[4:8], g0], axis=0)
        o_ei[:, layer] = jnp.where(is_even, even, odd)
        o_eo[layer] = jnp.where(is_even, g1[4:8], g1[0:4])

    def node_rows(layer, total):
        o_ni[layer] = total[0:8]
        last = total[8:16]
        o_no[layer] = jnp.where(is_even, last[0:4], last[4:8])
        return jnp.where(is_even, last[4:8], last[0:4])

    def four(row):
        lane = iota((1, D), 1)
        at = iota((1, 4), 1)
        picked = jnp.zeros((1, 4), F32)
        for i in range(4):
            value = jnp.sum(jnp.where(lane == column + i, row, 0.0), axis=1, keepdims=True)
            picked = jnp.where(at == i, value, picked)
        return picked

    def rows(start, size):
        return sums[SUMS_AT + start : SUMS_AT + start + size]

    edge_rows(1, rows(0, 8), rows(8, 8))
    edge_rows(0, rows(48, 8), rows(56, 8))
    gains = node_rows(1, rows(16, 16))
    o_eg[1:2] = four(gains[0:1])
    o_ng[1:2] = four(gains[1:2])
    o_ng[0:1] = four(node_rows(0, rows(32, 16))[0:1])
    last = rows(64, 8)
    o_eg[0:1] = four(jnp.concatenate([last[i : i + 1, 0:128] for i in range(4)], axis=1))


def body(*args):
    (node_latent, edge_latent, node_cotangent, ewi, ewo, nwi, nwo, *gains, edge_slot, edge_receiver, send_list, edge_count) = args
    vmem = pl.BlockSpec(memory_space=pltpu.VMEM)
    far = pl.BlockSpec(memory_space=pl.ANY)
    results = pl.pallas_call(
        kernel,
        out_shape=jax.ShapeDtypeStruct((SUMS_AT + 72, D), F32),
        in_specs=[far] * 8 + [vmem] * 5,
        out_specs=vmem,
        scratch_shapes=flat_scratch()[0],
        compiler_params=pltpu.CompilerParams(
            collective_id=0, has_side_effects=True, vmem_limit_bytes=VMEM_LIMIT
        ),
        cost_estimate=pl.CostEstimate(flops=10**10, bytes_accessed=10**7, transcendentals=10**6),
    )(
        node_latent[0],
        edge_latent[0],
        ewi,
        ewo,
        nwi,
        nwo,
        node_cotangent[0],
        edge_count,
        *gains,
        edge_slot.reshape(8, 128),
        edge_receiver.reshape(8, 128),
        send_list,
    )
    outs = (
        (NODES, D),
        (NODES, D),
        (12, 2, D),
        (2, 4, D),
        (2, 8, D),
        (2, 4, D),
        (2, 4),
        (2, 4),
    )
    results = pl.pallas_call(
        finish_kernel,
        out_shape=tuple(jax.ShapeDtypeStruct(shape, F32) for shape in outs),
        in_specs=[vmem],
        out_specs=tuple([vmem] * 8),
        compiler_params=pltpu.CompilerParams(vmem_limit_bytes=VMEM_LIMIT),
    )(results)
    return (results[0][None], results[1][None], jnp.transpose(results[2], (1, 0, 2))) + tuple(results[3:])


def solution(mesh):
    nodes = P(AXES[1], AXES[0], None)
    graph = P(AXES[0])
    in_specs = (nodes, nodes, nodes) + (P(),) * 6 + (graph, graph, P(AXES[0], None), graph)
    rows = P(None, AXES, None)
    out_specs = (nodes, nodes) + (rows,) * 4 + (P(None, AXES),) * 2
    return jax.shard_map(body, mesh=mesh, in_specs=in_specs, out_specs=out_specs, check_vma=False)
```

profile of v0, /device:TPU:0, one launch (start us, length us, event | category | flops | bytes accessed | tf_op | source)
XLA Modules:
  0.0 67.1 jit_solution(6175930319346758256)
XLA Ops:
  1.3 63.9 %shard_map.188.sums = f32[328,512]{1,0:T(8,128)} custom-call(bf16[128,512]{1,0:T(8,128)(2,1)} %bitcast.11, bf16[1024,512]{1,0:T(8,128)(2,1)} %bitcast.8, bf16[2,1536,512]{2,1,0:T(8,128)(2,1)} %refs_2_.1, bf16[2,512,512]{2,1,0:T(8,128)(2,1)} %refs_3_.1, bf16[2,1024,512]{2,1,0:T(8,128)(2,1)} %refs_4_.1, bf16[2,512,512]{2,1,0:T(8,128)(2,1)} %refs_5_.1, ...), custom_call_target="tpu_custom_call" | custom-call | flops 10000000000 | bytes 10000000 | tf_op jit(solution)/shard_map/pallas_call | solution.py:704
  65.1 2.0 %shard_map.189 = (f32[128,512]{1,0:T(8,128)}, f32[128,512]{1,0:T(8,128)}, f32[12,2,512]{2,1,0:T(2,128)}, f32[2,4,512]{2,1,0:T(4,128)}, f32[2,8,512]{2,1,0:T(8,12...) custom-call(f32[328,512]{1,0:T(8,128)} %shard_map.188.sums), custom_call_target="tpu_custom_call" | custom-call | tf_op jit(solution)/shard_map/pallas_call | solution.py:738
where the time goes:
time: 67.3 us; the launch traced here: 67.1 us
  Pallas kernels  65.8 us (98%)
  between operations  1.29 us (2%)
    pallas_call x1, Pallas kernels, body(): pl.pallas_call(kernel, out_shape=jax.ShapeDtypeStruct((SUMS_AT + 72, D),...  63.9 us
    pallas_call x1, Pallas kernels, body(): pl.pallas_call(finish_kernel, out_shape=tuple((jax.ShapeDtypeStruct(shape...  1.97 us

commit v1 on v0

--- a/solution.py
+++ b/solution.py
@@ -23,10 +23,14 @@
 RECV_AT = NODES
 HALO_AT = 2 * NODES
 SUMS_AT = 2 * NODES
-FIRST, FORE, BACK = 1024, 1024, 512
+FIRST, FORE, BACK = 1024, 1024, 1024
 FORE_UNROLL, BACK_UNROLL = 1, 1
 MESH = pl.DeviceIdType.MESH
-STREAM_TILES = (((16, 512),) * 3, ((8, 384), (8, 384), (24, 128)))
+STREAM_TILES = (
+    ((16, 384), (16, 384), (32, 128)),
+    ((8, 384), (8, 384), (16, 128)),
+    ((8, 384), (8, 384), (24, 128)),
+)
 PART_ORDER = ((1, 2, 0), (2, 0, 1), (0, 1, 2))
 AXES = ("graph", "batch")
 scope = jax.named_scope
@@ -74,7 +78,7 @@
         return [vm(shape, dtype), vm(shape, dtype)]
 
     def parts(shape):
-        keys = [(stream, part) for stream in range(2) for part in range(3)]
+        keys = [(stream, part) for stream in range(3) for part in range(3)]
         return {key: vm(shape(key[1]) + STREAM_TILES[key[0]][key[1]], BF) for key in keys}
 
     return dict(
@@ -86,6 +90,13 @@
         nwo=vm((2, D, D), BF),
         cot=vm((NODES, D), BF),
         cnt=pltpu.SMEM((1,), jnp.int32),
+        small=[
+            vm((2, D), F32),
+            vm((2, D), F32),
+            vm((8, 128), jnp.int32),
+            vm((8, 128), jnp.int32),
+            vm((GROUP, PEER), jnp.int32),
+        ],
         SR=vm((EDGES, 512), BF),
         SRT=vm((512, EDGES), BF),
         LT=vm((NODES, HALO), BF),
@@ -94,6 +105,7 @@
         EB1=vm((EDGES, D), BF),
         VB1=vm((NODES, D), BF),
         V1=vm((NODES, D), F32),
+        NPRE=vm((NODES, D), F32),
         N=two((EDGES, D), BF),
         DA=two((EDGES, D), BF),
         H=two((EDGES, D), BF),
@@ -117,7 +129,6 @@
         RD=parts(lambda part: (3,)),
         GZ=vm((EDGES, D), BF),
         GA=vm((EDGES, D), BF),
-        GE=vm((EDGES, D), F32),
         GSR=vm((HALO_AT, D), F32),
         GV=vm((NODES, D), F32),
         GACC=vm((8, D), F32),
@@ -125,11 +136,13 @@
         WEO=vm((D, D), F32),
         WN=vm((2 * D, D), F32),
         WNO=vm((D, D), F32),
-        load=pltpu.SemaphoreType.DMA((12,)),
+        OUT=vm((SUMS_AT + 72, D), F32),
+        store=pltpu.SemaphoreType.DMA((3,)),
+        load=pltpu.SemaphoreType.DMA((17,)),
         halo_send=pltpu.SemaphoreType.DMA((2, 2, 5)),
         halo_recv=pltpu.SemaphoreType.DMA((2, 2, 5)),
-        rs_send=pltpu.SemaphoreType.DMA((2, 3, 13)),
-        rs_recv=pltpu.SemaphoreType.DMA((2, 3, 13)),
+        rs_send=pltpu.SemaphoreType.DMA((3, 3, 13)),
+        rs_recv=pltpu.SemaphoreType.DMA((3, 3, 13)),
     )
 
 
@@ -138,7 +151,7 @@
 
 
 def kernel(*refs):
-    far, (eg, ng, slot, rcv, slist), (out,) = refs[:8], refs[8:13], refs[13:14]
+    far, out = refs[:13], refs[13]
     r = types.SimpleNamespace(**jax.tree.unflatten(flat_scratch()[1], refs[14:]))
     g = lax.axis_index(AXES[0])
     y = lax.axis_index(AXES[1])
@@ -171,9 +184,11 @@
     pl.semaphore_signal(barrier, inc=1, device_id=other_core, device_id_type=MESH)
     greeted += 1
 
-    nl, el, ewi, ewo, nwi, nwo, cot, cnt = far
+    nl, el, ewi, ewo, nwi, nwo, cot, cnt, *small = far
     pairs = [(nl, r.nl), (ewi, r.ewi, 0), (el, r.el), (ewo, r.ewo, 0), (nwi, r.nwi, 0), (nwo, r.nwo, 0)]
     pairs += [(ewi, r.ewi, 1), (ewo, r.ewo, 1), (nwi, r.nwi, 1), (nwo, r.nwo, 1), (cot, r.cot), (cnt, r.cnt)]
+    eg, ng, slot, rcv, slist = r.small
+    pairs += list(zip(small, r.small))
 
     def load(number):
         src, dst, *layer = pairs[number]
@@ -181,9 +196,10 @@
             src, dst = src.at[layer[0]], dst.at[layer[0]]
         return pltpu.make_async_copy(src, dst, r.load.at[number])
 
-    for number in (11,) + tuple(range(11)):
+    for number in (16, 0, 14, 15, 11) + tuple(range(1, 11)) + (12, 13):
         load(number).start()
 
+    load(16).wait()
     listed = jnp.concatenate(
         [slist[pl.ds(wrap(g - offset, GROUP), 1), :] for offset in OFFSETS], axis=1
     ).astype(F32)
@@ -216,7 +232,8 @@
         return r.el if layer == 0 else r.EB1
 
     def one_hots():
-        load(11).wait()
+        for number in (11, 14, 15):
+            load(number).wait()
         s = slot[...]
         within = s - NODES
         source = within // PEER
@@ -264,7 +281,6 @@
         wo = r.ewo.at[layer]
         nw = r.nwi.at[layer]
         nwo = r.nwo.at[layer]
-        gain = eg[layer : layer + 1, :]
         ps = r.PS
         with scope("f_send"):
             if layer == 0:
@@ -292,13 +308,18 @@
                 return carry
 
             lax.fori_loop(0, EDGES // FIRST, first, 0)
+            load(NWI[layer]).wait()
+            r.NPRE[...] = dot(node, nw[0:D])
         with scope("f_halo_wait"):
             load(EWO[layer]).wait()
-            load(NWI[layer]).wait()
             load(NWO[layer]).wait()
             for copy in copies:
                 copy.wait()
         with scope("f_edges"):
+            if layer == 0:
+                load(12).wait()
+                load(13).wait()
+            gain = eg[layer : layer + 1, :]
             ps[HALO_AT : HALO_AT + HALO] = dot(r.HR[layer][...], w[D : 2 * D]).astype(BF)
 
             def edges(t, carry):
@@ -319,7 +340,7 @@
         with scope("f_node"):
             agg = (dot(r.SRT[RECV_AT:HALO_AT], r.N[layer][...]) * gain).astype(BF)
             r.AGG[layer][...] = agg
-            pre_act = dot(node, nw[0:D]) + dot(agg, nw[D:])
+            pre_act = r.NPRE[...] + dot(agg, nw[D:])
             hidden, slope = swish(pre_act)
             hidden = hidden.astype(BF)
             r.NH[layer][...] = hidden
@@ -333,7 +354,7 @@
                 r.V1[...] = state
                 r.VB1[...] = state.astype(BF)
             else:
-                out[0:NODES] = r.V1[...] + update
+                r.OUT[0:NODES] = r.V1[...] + update
 
     def norm_back(grad, normed, inv_std):
         return inv_std * (
@@ -355,7 +376,6 @@
             gz = norm_back(grad * ng[layer : layer + 1, :], normed, r.NINV[layer][...]).astype(BF)
             ga = (dot_tb(gz, r.nwo[layer]) * r.NDA[layer][...]).astype(BF)
             grad_agg = dot_tb(ga, nw[D:]).astype(BF)
-            r.GV[...] = grad + dot_tb(ga, nw[0:D])
             r.GACC[...] = jnp.zeros((8, D), F32)
 
         def weights():
@@ -363,11 +383,11 @@
                 r.WN[0:D] = dot_ta(node, ga)
                 r.WN[D:] = dot_ta(r.AGG[layer][...], ga)
                 r.WNO[...] = dot_ta(r.NH[layer][...], gz)
+                r.GV[...] = r.GV[...] + dot_tb(ga, nw[0:D])
 
         return grad_agg, gain_sum, weights
 
-    def backward_edges(layer, grad_agg, begin, end):
-        w = r.ewi.at[layer]
+    def backward_edges(layer, grad_agg):
         wo = r.ewo.at[layer]
         gain = eg[layer : layer + 1, :]
 
@@ -375,19 +395,17 @@
             at = tile_at(t, BACK)
             gm = dot(r.SR[at, RECV_AT:HALO_AT], grad_agg)
             if layer == 0:
-                gm = gm + r.GE[at]
+                gm = gm + r.PRE[at]
             en = r.N[layer][at].astype(F32)
             r.GACC[...] += fold_rows(gm * en)
             ez = norm_back(gm * gain, en, r.INV[layer][at]).astype(BF)
             r.GZ[at] = ez
             ea = (dot_tb(ez, wo[...]) * r.DA[layer][at].astype(F32)).astype(BF)
             r.GA[at] = ea
-            if layer == 1:
-                r.GE[at] = dot_tb(ea, w[0:D])
             return carry
 
         with scope("b_edges"):
-            lax.fori_loop(begin, end, edges, 0, unroll=BACK_UNROLL)
+            lax.fori_loop(0, EDGES // BACK, edges, 0, unroll=BACK_UNROLL)
 
     def return_halo(layer):
         with scope("b_gsr"):
@@ -410,6 +428,13 @@
             r.WE[2 * D :] = dot_ta(node, to_receiver)
         return jnp.sum(r.GACC[...], axis=0, keepdims=True)
 
+    def edge_inputs(layer):
+        with scope("b_inputs"):
+            to_receiver = r.GSR[RECV_AT:HALO_AT].astype(BF)
+            r.GV[...] = r.GV[...] + dot_tb(to_receiver, r.ewi[layer, 2 * D :])
+            if layer == 1:
+                r.PRE[...] = dot_tb(r.GA[...], r.ewi[layer, 0:D])
+
     def take_halo(layer, copies):
         w = r.ewi.at[layer]
         with scope("b_halo_wait"):
@@ -417,8 +442,7 @@
                 copy.wait()
         with scope("b_tail"):
             to_sender = (r.GSR[0:NODES] + dot(r.LT[...], r.BR[layer][...])).astype(BF)
-            to_receiver = r.GSR[RECV_AT:HALO_AT].astype(BF)
-            total = r.GV[...] + dot_tb(to_sender, w[D : 2 * D]) + dot_tb(to_receiver, w[2 * D :])
+            total = r.GV[...] + dot_tb(to_sender, w[D : 2 * D])
             r.GV[...] = total
         return total
 
@@ -448,11 +472,13 @@
             for odd, (g0, g1) in enumerate(edge_slots(k)):
                 at = where + (yy + odd,)
                 if layer == 1:
-                    r.G[0, 0][at] = jnp.concatenate([g0, g1], axis=0).astype(BF)
+                    both = jnp.concatenate([g0, g1], axis=0).astype(BF)
+                    r.G[0, 0][at] = both[:, 0:384]
+                    r.G[0, 2][at + (slice(0, 16),)] = both[:, 384:]
                 else:
-                    r.G[1, 0][at] = g0[:, 0:384].astype(BF)
-                    r.G[1, 1][at] = g1[:, 0:384].astype(BF)
-                    r.G[1, 2][at] = jnp.concatenate([g0[:, 384:], g1[:, 384:], gains], axis=0).astype(BF)
+                    r.G[2, 0][at] = g0[:, 0:384].astype(BF)
+                    r.G[2, 1][at] = g1[:, 0:384].astype(BF)
+                    r.G[2, 2][at] = jnp.concatenate([g0[:, 384:], g1[:, 384:], gains], axis=0).astype(BF)
 
         if layer == 0:
             lanes = [gain_sum[:, 128 * i : 128 * (i + 1)] for i in range(4)]
@@ -467,15 +493,20 @@
         gains = jnp.zeros((8, D), F32)
         for i, gain_sum in enumerate(gain_sums):
             gains = jnp.where(row == i, gain_sum, gains)
-        target = r.G[0, 1] if layer == 1 else r.G[0, 2]
-
         def pair(where, yy, k):
             n0, n1 = (pair_rows(r.WN, k, 8 * i, 16) for i in range(2))
             last = pair_rows(r.WNO, k, 0, 8)
-            even = jnp.concatenate([n0, jnp.where(low, last, gains)], axis=0)
-            odd = jnp.concatenate([n1, jnp.where(low, gains, last)], axis=0)
-            target[where + (yy,)] = even.astype(BF)
-            target[where + (yy + 1,)] = odd.astype(BF)
+            slots = ((n0, jnp.where(low, last, gains)), (n1, jnp.where(low, gains, last)))
+            for odd, (g2, g3) in enumerate(slots):
+                at = where + (yy + odd,)
+                if layer == 1:
+                    both = jnp.concatenate([g2, g3], axis=0).astype(BF)
+                    r.G[0, 1][at] = both[:, 0:384]
+                    r.G[0, 2][at + (slice(16, 32),)] = both[:, 384:]
+                else:
+                    r.G[1, 0][at] = g2[:, 0:384].astype(BF)
+                    r.G[1, 1][at] = g3[:, 0:384].astype(BF)
+                    r.G[1, 2][at] = jnp.concatenate([g2[:, 384:], g3[:, 384:]], axis=0).astype(BF)
 
         with scope("asm_nodes"):
             each_pair(pair)
@@ -593,67 +624,72 @@
             for i in range(3):
                 total = total + r.RD[key][i].astype(F32)
             stream, part = key
-            if stream == 0:
-                out[SUMS_AT + 16 * part : SUMS_AT + 16 * part + 16] = total
-            elif part < 2:
-                out[SUMS_AT + 48 + 8 * part : SUMS_AT + 56 + 8 * part, 0:384] = total
+            start = SUMS_AT + (0, 32, 48)[stream]
+            rows = 16 if stream == 0 else 8
+            if part < 2:
+                r.OUT[start + rows * part : start + rows * part + rows, 0:384] = total
             else:
-                for i in range(2):
-                    out[SUMS_AT + 48 + 8 * i : SUMS_AT + 56 + 8 * i, 384:] = total[8 * i : 8 * i + 8]
-                out[SUMS_AT + 64 :, 0:128] = total[16:24]
-
-    early = ((0, 0), (0, 1), (0, 2))
-    late = ((1, 0), (1, 1), (1, 2))
-
-    def each(call, keys):
-        for key in keys:
-            call(key)
+                r.OUT[start : start + 2 * rows, 384:] = total[0 : 2 * rows]
+            if key == (2, 2):
+                r.OUT[SUMS_AT + 64 :, 0:128] = total[16:24]
+
+    def store(number):
+        rows = pl.ds((0, NODES, SUMS_AT)[number], (NODES, NODES, 72)[number])
+        return pltpu.make_async_copy(r.OUT.at[rows], out.at[rows], r.store.at[number])
+
+    def each(call, stream, *parts):
+        for part in parts or range(3):
+            call((stream, part))
 
     forward(0)
     forward(1)
+    store(0).start()
     load(COT).wait()
     r.GV[...] = r.cot[...].astype(F32)
-    count = EDGES // BACK
 
     grad_agg, node_gain, node_weights = backward_nodes(1)
-    backward_edges(1, grad_agg, 0, count)
+    backward_edges(1, grad_agg)
     copies = return_halo(1)
     edge_gain = edge_weights(1)
     assemble_edges(1, None)
-    rs_cores((0, 0))
+    each(rs_cores, 0, 0)
+    edge_inputs(1)
     node_weights()
     assemble_nodes(1, edge_gain, node_gain)
-    rs_cores((0, 1))
+    each(rs_cores, 0, 1, 2)
     take_halo(1, copies)
-    rs_ring((0, 0))
+    each(rs_ring, 0, 0)
 
     grad_agg, node_gain, node_weights = backward_nodes(0)
     node_weights()
     assemble_nodes(0, node_gain)
-    rs_cores((0, 2))
-    rs_ring((0, 1))
-    backward_edges(0, grad_agg, 0, count)
-    rs_ring((0, 2))
+    each(rs_cores, 1)
+    each(rs_ring, 0, 1, 2)
+    backward_edges(0, grad_agg)
     copies = return_halo(0)
-    rs_sums((0, 0))
+    each(rs_ring, 1)
+    each(rs_sums, 0, 0)
     edge_gain = edge_weights(0)
-    rs_sums((0, 1))
     assemble_edges(0, edge_gain)
-    each(rs_cores, late)
-    rs_sums((0, 2))
-    each(rs_ring, late)
-    out[NODES : 2 * NODES] = take_halo(0, copies)
-    rs_second((0, 0))
-    each(rs_sums, late)
-    rs_second((0, 1))
-    rs_second((0, 2))
-    rs_third((0, 0))
-    each(rs_second, late)
-    rs_third((0, 1))
-    rs_third((0, 2))
-    each(rs_third, late)
-    each(rs_finish, early)
-    each(rs_finish, late)
+    each(rs_cores, 2)
+    each(rs_sums, 0, 1, 2)
+    edge_inputs(0)
+    each(rs_ring, 2)
+    each(rs_sums, 1)
+    each(rs_second, 0)
+    each(rs_sums, 2)
+    each(rs_second, 1)
+    r.OUT[NODES : 2 * NODES] = take_halo(0, copies)
+    store(1).start()
+    each(rs_third, 0)
+    each(rs_second, 2)
+    each(rs_third, 1)
+    each(rs_third, 2)
+    for stream in range(3):
+        each(rs_finish, stream)
+    store(2).start()
+    for number in range(3):
+        store(number).wait()
 
 
 def finish_kernel(sums, o_node, o_grad, o_ei, o_eo, o_ni, o_no, o_eg, o_ng):
@@ -704,8 +740,8 @@
     results = pl.pallas_call(
         kernel,
         out_shape=jax.ShapeDtypeStruct((SUMS_AT + 72, D), F32),
-        in_specs=[far] * 8 + [vmem] * 5,
-        out_specs=vmem,
+        in_specs=[far] * 13,
+        out_specs=far,
         scratch_shapes=flat_scratch()[0],
         compiler_params=pltpu.CompilerParams(
             collective_id=0, has_side_effects=True, vmem_limit_bytes=VMEM_LIMIT

time: 67.3 us -> 64.1 us (0.952)
  Pallas kernels: 65.8 us -> 62.7 us
    pallas_call x1, Pallas kernels: 63.9 us -> 60.7 us  [body(): pl.pallas_call(kernel, out_shape=jax.ShapeDtypeStruct((SUMS_AT + 72, D),...]
where the time goes in v1:
time: 64.1 us; the launch traced here: 64 us
  Pallas kernels  62.7 us (98%)
  between operations  1.29 us (2%)
    pallas_call x1, Pallas kernels, body(): pl.pallas_call(kernel, out_shape=jax.ShapeDtypeStruct((SUMS_AT + 72, D),...  60.7 us
    pallas_call x1, Pallas kernels, body(): pl.pallas_call(finish_kernel, out_shape=tuple((jax.ShapeDtypeStruct(shape...  1.97 us

profile of v1, /device:TPU:0, one launch (start us, length us, event | category | flops | bytes accessed | tf_op | source)
XLA Modules:
  0.0 64.0 jit_solution(3389200596701051956)
XLA Ops:
  1.3 60.7 %shard_map.188.sums = f32[328,512]{1,0:T(8,128)} custom-call(bf16[128,512]{1,0:T(8,128)(2,1)} %bitcast.11, bf16[1024,512]{1,0:T(8,128)(2,1)} %bitcast.8, bf16[2,1536,512]{2,1,0:T(8,128)(2,1)} %refs_2_.1, bf16[2,512,512]{2,1,0:T(8,128)(2,1)} %refs_3_.1, bf16[2,1024,512]{2,1,0:T(8,128)(2,1)} %refs_4_.1, bf16[2,512,512]{2,1,0:T(8,128)(2,1)} %refs_5_.1, ...), custom_call_target="tpu_custom_call" | custom-call | flops 10000000000 | bytes 10000000 | tf_op jit(solution)/shard_map/pallas_call | solution.py:740
  62.0 2.0 %shard_map.189 = (f32[128,512]{1,0:T(8,128)}, f32[128,512]{1,0:T(8,128)}, f32[12,2,512]{2,1,0:T(2,128)}, f32[2,4,512]{2,1,0:T(4,128)}, f32[2,8,512]{2,1,0:T(8,12...) custom-call(f32[328,512]{1,0:T(8,128)} %shard_map.188.sums), custom_call_target="tpu_custom_call" | custom-call | tf_op jit(solution)/shard_map/pallas_call | solution.py:774

commit v2 on v1

--- a/solution.py
+++ b/solution.py
@@ -139,10 +139,10 @@
         OUT=vm((SUMS_AT + 72, D), F32),
         store=pltpu.SemaphoreType.DMA((3,)),
         load=pltpu.SemaphoreType.DMA((17,)),
-        halo_send=pltpu.SemaphoreType.DMA((2, 2, 5)),
-        halo_recv=pltpu.SemaphoreType.DMA((2, 2, 5)),
-        rs_send=pltpu.SemaphoreType.DMA((3, 3, 13)),
-        rs_recv=pltpu.SemaphoreType.DMA((3, 3, 13)),
+        halo_send=pltpu.SemaphoreType.DMA((2, 2)),
+        halo_recv=pltpu.SemaphoreType.DMA((2, 2)),
+        rs_send=pltpu.SemaphoreType.DMA((3, 3, 5)),
+        rs_recv=pltpu.SemaphoreType.DMA((3, 3, 5)),
     )
 
 
@@ -206,6 +206,16 @@
     node_ids = iota((NODES, HALO), 0).astype(F32)
     r.LT[...] = jnp.where(node_ids == listed, 1.0, 0.0).astype(BF)
 
+    def remote(src, dst, send_sem, recv_sem, device):
+        return pltpu.make_async_remote_copy(
+            src_ref=src,
+            dst_ref=dst,
+            send_sem=send_sem,
+            recv_sem=recv_sem,
+            device_id=device,
+            device_id_type=MESH,
+        )
+
     def halo_copies(layer, way):
         src, dst = ((r.HS, r.HR), (r.BS, r.BR))[way]
         src, dst = src[layer], dst[layer]
@@ -214,16 +224,15 @@
             offset = OFFSETS[b]
             rows = pl.ds(b * PEER, PEER)
             copies.append(
-                pltpu.make_async_remote_copy(
-                    src_ref=src.at[rows],
-                    dst_ref=dst.at[rows],
-                    send_sem=r.halo_send.at[layer, way, b],
-                    recv_sem=r.halo_recv.at[layer, way, b],
-                    device_id=graph_peer(-offset if way == 0 else offset),
-                    device_id_type=MESH,
+                remote(
+                    src.at[rows],
+                    dst.at[rows],
+                    r.halo_send.at[layer, way],
+                    r.halo_recv.at[layer, way],
+                    graph_peer(-offset if way == 0 else offset),
                 )
             )
-        return copies
+        return copies, remote(src, dst, r.halo_send.at[layer, way], r.halo_recv.at[layer, way], other_core)
 
     def vb(layer):
         return r.nl if layer == 0 else r.VB1
@@ -286,7 +295,7 @@
             if layer == 0:
                 load(NL).wait()
             r.HS[layer][...] = dot_ta(r.LT[...], vb(layer)[...]).astype(BF)
-            copies = halo_copies(layer, 0)
+            copies, all_rows = halo_copies(layer, 0)
             if layer == 0:
                 pl.semaphore_wait(barrier, greeted)
             for copy in copies:
@@ -313,8 +322,7 @@
         with scope("f_halo_wait"):
             load(EWO[layer]).wait()
             load(NWO[layer]).wait()
-            for copy in copies:
-                copy.wait()
+            all_rows.wait()
         with scope("f_edges"):
             if layer == 0:
                 load(12).wait()
@@ -412,10 +420,10 @@
             sums = dot(r.SRT[...], r.GA[...])
             r.GSR[...] = sums[0:HALO_AT]
             r.BS[layer][...] = sums[HALO_AT : HALO_AT + HALO].astype(BF)
-            copies = halo_copies(layer, 1)
+            copies, all_rows = halo_copies(layer, 1)
             for copy in copies:
                 copy.start()
-        return copies
+        return all_rows
 
     def edge_weights(layer):
         node = vb(layer)[...]
@@ -438,8 +446,7 @@
     def take_halo(layer, copies):
         w = r.ewi.at[layer]
         with scope("b_halo_wait"):
-            for copy in copies:
-                copy.wait()
+            copies.wait()
         with scope("b_tail"):
             to_sender = (r.GSR[0:NODES] + dot(r.LT[...], r.BR[layer][...])).astype(BF)
             total = r.GV[...] + dot_tb(to_sender, w[D : 2 * D])
@@ -512,14 +519,10 @@
             each_pair(pair)
 
     def rs_copy(key, number, src, dst, device):
-        return pltpu.make_async_remote_copy(
-            src_ref=src,
-            dst_ref=dst,
-            send_sem=r.rs_send.at[key[0], key[1], number],
-            recv_sem=r.rs_recv.at[key[0], key[1], number],
-            device_id=device,
-            device_id_type=MESH,
-        )
+        return remote(src, dst, r.rs_send.at[key[0], key[1], number], r.rs_recv.at[key[0], key[1], number], device)
+
+    def settle(key, number, ref):
+        rs_copy(key, number, ref, ref, other_core).wait()
 
     def cores(key):
         return rs_copy(key, 0, r.G[key].at[:, :, 1 - core], r.RC[key], other_core)
@@ -546,14 +549,14 @@
             src = r.RC[key].at[cut(key, wrap(me + sign, 4), way)]
         else:
             src = r.CA[key].at[way]
-        return rs_copy(key, 1 + slot, src, r.RA[key].at[slot], peer(axis, sign))
+        return rs_copy(key, 1 if kind == 0 else 2, src, r.RA[key].at[slot], peer(axis, sign))
 
     def second_copies(key):
         _, axis, _, at = axes(key)
         copies = []
         for step in (2, 1, 3):
             src = r.AB[key].at[(slice(None),) * at + (wrap(place[axis] + step, 4),)]
-            copies.append(rs_copy(key, 6 + step, src, r.RB[key].at[step - 1], peer(axis, step)))
+            copies.append(rs_copy(key, 3, src, r.RB[key].at[step - 1], peer(axis, step)))
         return copies
 
     def third_copies(key):
@@ -561,7 +564,7 @@
         copies = []
         for step in (2, 1, 3):
             src = r.AD[key].at[wrap(place[axis] + step, 4)]
-            copies.append(rs_copy(key, 9 + step, src, r.RD[key].at[step - 1], peer(axis, step)))
+            copies.append(rs_copy(key, 4, src, r.RD[key].at[step - 1], peer(axis, step)))
         return copies
 
     def rs_cores(key):
@@ -583,18 +586,18 @@
     def rs_sums(key):
         with scope("rs_sums"):
             me = place[axes(key)[0]]
+            got = r.RA[key]
+            settle(key, 1, got.at[0:2])
             for way, sign in ((0, 1), (1, -1)):
-                ring(key, 3 * way).wait()
                 own = r.RC[key][cut(key, wrap(me + sign, 4), 1 - way)]
-                r.CA[key][way] = own + r.RA[key][3 * way]
+                r.CA[key][way] = own + got[3 * way]
                 ring(key, 3 * way + 2).start()
 
     def rs_second(key):
         with scope("rs_second"):
             first, axis, _, at = axes(key)
-            for slot in (1, 4, 2, 5):
-                ring(key, slot).wait()
             got = r.RA[key]
+            settle(key, 2, got.at[0:4])
             for half in range(2):
                 near, summed = (1, 5) if half == 0 else (4, 2)
                 total = r.RC[key][cut(key, place[first], half)].astype(F32)
@@ -607,8 +610,7 @@
     def rs_third(key):
         with scope("rs_third"):
             _, axis, _, at = axes(key)
-            for copy in second_copies(key):
-                copy.wait()
+            settle(key, 3, r.RB[key])
             total = r.AB[key][(slice(None),) * at + (place[axis],)].astype(F32)
             for i in range(3):
                 total = total + r.RB[key][i].astype(F32)
@@ -618,8 +620,7 @@
 
     def rs_finish(key):
         with scope("rs_finish"):
-            for copy in third_copies(key):
-                copy.wait()
+            settle(key, 4, r.RD[key])
             total = r.AD[key][place[axes(key)[2]]].astype(F32)
             for i in range(3):
                 total = total + r.RD[key][i].astype(F32)
@@ -687,9 +688,10 @@
     each(rs_third, 2)
     for stream in range(3):
         each(rs_finish, stream)
-    store(2).start()
-    for number in range(3):
-        store(number).wait()
+    with scope("z_store"):
+        store(2).start()
+        for number in range(3):
+            store(number).wait()
 
 
 def finish_kernel(sums, o_node, o_grad, o_ei, o_eo, o_ni, o_no, o_eg, o_ng):

time: 64.1 us -> 62.5 us (0.975)
  Pallas kernels: 62.7 us -> 61.1 us
    pallas_call x1, Pallas kernels: 60.7 us -> 59.1 us  [body(): pl.pallas_call(kernel, out_shape=jax.ShapeDtypeStruct((SUMS_AT + 72, D),...]
where the time goes in v2:
time: 62.5 us; the launch traced here: 62.4 us
  Pallas kernels  61.1 us (98%)
  between operations  1.29 us (2%)
    pallas_call x1, Pallas kernels, body(): pl.pallas_call(kernel, out_shape=jax.ShapeDtypeStruct((SUMS_AT + 72, D),...  59.1 us
    pallas_call x1, Pallas kernels, body(): pl.pallas_call(finish_kernel, out_shape=tuple((jax.ShapeDtypeStruct(shape...  1.97 us

profile of v2, /device:TPU:0, one launch (start us, length us, event | category | flops | bytes accessed | tf_op | source)
XLA Modules:
  0.0 62.4 jit_solution(9544636431962939826)
XLA Ops:
  1.3 59.1 %shard_map.188.sums = f32[328,512]{1,0:T(8,128)} custom-call(bf16[128,512]{1,0:T(8,128)(2,1)} %bitcast.11, bf16[1024,512]{1,0:T(8,128)(2,1)} %bitcast.8, bf16[2,1536,512]{2,1,0:T(8,128)(2,1)} %refs_2_.1, bf16[2,512,512]{2,1,0:T(8,128)(2,1)} %refs_3_.1, bf16[2,1024,512]{2,1,0:T(8,128)(2,1)} %refs_4_.1, bf16[2,512,512]{2,1,0:T(8,128)(2,1)} %refs_5_.1, ...), custom_call_target="tpu_custom_call" | custom-call | flops 10000000000 | bytes 10000000 | tf_op jit(solution)/shard_map/pallas_call | solution.py:742
  60.4 2.0 %shard_map.189 = (f32[128,512]{1,0:T(8,128)}, f32[128,512]{1,0:T(8,128)}, f32[12,2,512]{2,1,0:T(2,128)}, f32[2,4,512]{2,1,0:T(4,128)}, f32[2,8,512]{2,1,0:T(8,12...) custom-call(f32[328,512]{1,0:T(8,128)} %shard_map.188.sums), custom_call_target="tpu_custom_call" | custom-call | tf_op jit(solution)/shard_map/pallas_call | solution.py:776

commit v3 on v2

--- a/solution.py
+++ b/solution.py
@@ -171,6 +171,21 @@
 
     other_core = place_id(g + 1 - 2 * core, y)
 
+    nl, el, ewi, ewo, nwi, nwo, cot, cnt, *small = far
+    pairs = [(nl, r.nl), (ewi, r.ewi, 0), (el, r.el), (ewo, r.ewo, 0), (nwi, r.nwi, 0), (nwo, r.nwo, 0)]
+    pairs += [(ewi, r.ewi, 1), (ewo, r.ewo, 1), (nwi, r.nwi, 1), (nwo, r.nwo, 1), (cot, r.cot), (cnt, r.cnt)]
+    eg, ng, slot, rcv, slist = r.small
+    pairs += list(zip(small, r.small))
+
+    def load(number):
+        src, dst, *layer = pairs[number]
+        if layer:
+            src, dst = src.at[layer[0]], dst.at[layer[0]]
+        return pltpu.make_async_copy(src, dst, r.load.at[number])
+
+    for number in (16, 0):
+        load(number).start()
+
     barrier = pltpu.get_barrier_semaphore()
     greeted = 0
     for offset in OFFSETS:
@@ -184,19 +199,7 @@
     pl.semaphore_signal(barrier, inc=1, device_id=other_core, device_id_type=MESH)
     greeted += 1
 
-    nl, el, ewi, ewo, nwi, nwo, cot, cnt, *small = far
-    pairs = [(nl, r.nl), (ewi, r.ewi, 0), (el, r.el), (ewo, r.ewo, 0), (nwi, r.nwi, 0), (nwo, r.nwo, 0)]
-    pairs += [(ewi, r.ewi, 1), (ewo, r.ewo, 1), (nwi, r.nwi, 1), (nwo, r.nwo, 1), (cot, r.cot), (cnt, r.cnt)]
-    eg, ng, slot, rcv, slist = r.small
-    pairs += list(zip(small, r.small))
-
-    def load(number):
-        src, dst, *layer = pairs[number]
-        if layer:
-            src, dst = src.at[layer[0]], dst.at[layer[0]]
-        return pltpu.make_async_copy(src, dst, r.load.at[number])
-
-    for number in (16, 0, 14, 15, 11) + tuple(range(1, 11)) + (12, 13):
+    for number in (14, 15, 11) + tuple(range(1, 11)) + (12, 13):
         load(number).start()
 
     load(16).wait()
@@ -654,14 +657,14 @@
     edge_gain = edge_weights(1)
     assemble_edges(1, None)
     each(rs_cores, 0, 0)
-    edge_inputs(1)
     node_weights()
     assemble_nodes(1, edge_gain, node_gain)
     each(rs_cores, 0, 1, 2)
+    edge_inputs(1)
     take_halo(1, copies)
+
+    grad_agg, node_gain, node_weights = backward_nodes(0)
     each(rs_ring, 0, 0)
-
-    grad_agg, node_gain, node_weights = backward_nodes(0)
     node_weights()
     assemble_nodes(0, node_gain)
     each(rs_cores, 1)
@@ -669,11 +672,10 @@
     backward_edges(0, grad_agg)
     copies = return_halo(0)
     each(rs_ring, 1)
-    each(rs_sums, 0, 0)
     edge_gain = edge_weights(0)
     assemble_edges(0, edge_gain)
     each(rs_cores, 2)
-    each(rs_sums, 0, 1, 2)
+    each(rs_sums, 0)
     edge_inputs(0)
     each(rs_ring, 2)
     each(rs_sums, 1)

time: 62.5 us -> 62.1 us (level)
  no operation moved by 1% of the time
where the time goes in v3:
time: 62.1 us; the launch traced here: 62 us
  Pallas kernels  60.7 us (98%)
  between operations  1.29 us (2%)
    pallas_call x1, Pallas kernels, body(): pl.pallas_call(kernel, out_shape=jax.ShapeDtypeStruct((SUMS_AT + 72, D),...  58.7 us
    pallas_call x1, Pallas kernels, body(): pl.pallas_call(finish_kernel, out_shape=tuple((jax.ShapeDtypeStruct(shape...  1.97 us

profile of v3, /device:TPU:0, one launch (start us, length us, event | category | flops | bytes accessed | tf_op | source)
XLA Modules:
  0.0 62.0 jit_solution(9896157038816810752)
XLA Ops:
  1.3 58.7 %shard_map.188.sums = f32[328,512]{1,0:T(8,128)} custom-call(bf16[128,512]{1,0:T(8,128)(2,1)} %bitcast.11, bf16[1024,512]{1,0:T(8,128)(2,1)} %bitcast.8, bf16[2,1536,512]{2,1,0:T(8,128)(2,1)} %refs_2_.1, bf16[2,512,512]{2,1,0:T(8,128)(2,1)} %refs_3_.1, bf16[2,1024,512]{2,1,0:T(8,128)(2,1)} %refs_4_.1, bf16[2,512,512]{2,1,0:T(8,128)(2,1)} %refs_5_.1, ...), custom_call_target="tpu_custom_call" | custom-call | flops 10000000000 | bytes 10000000 | tf_op jit(solution)/shard_map/pallas_call | solution.py:744
  60.0 2.0 %shard_map.189 = (f32[128,512]{1,0:T(8,128)}, f32[128,512]{1,0:T(8,128)}, f32[12,2,512]{2,1,0:T(2,128)}, f32[2,4,512]{2,1,0:T(4,128)}, f32[2,8,512]{2,1,0:T(8,12...) custom-call(f32[328,512]{1,0:T(8,128)} %shard_map.188.sums), custom_call_target="tpu_custom_call" | custom-call | tf_op jit(solution)/shard_map/pallas_call | solution.py:778

commit v4 on v3

--- a/solution.py
+++ b/solution.py
@@ -141,7 +141,7 @@
         load=pltpu.SemaphoreType.DMA((17,)),
         halo_send=pltpu.SemaphoreType.DMA((2, 2)),
         halo_recv=pltpu.SemaphoreType.DMA((2, 2)),
-        rs_send=pltpu.SemaphoreType.DMA((3, 3, 5)),
+        rs_send=pltpu.SemaphoreType.DMA((3, 3, 4)),
         rs_recv=pltpu.SemaphoreType.DMA((3, 3, 5)),
     )
 
@@ -522,7 +522,8 @@
             each_pair(pair)
 
     def rs_copy(key, number, src, dst, device):
-        return remote(src, dst, r.rs_send.at[key[0], key[1], number], r.rs_recv.at[key[0], key[1], number], device)
+        sent = (0, 1, 1, 2, 3)[number]
+        return remote(src, dst, r.rs_send.at[key[0], key[1], sent], r.rs_recv.at[key[0], key[1], number], device)
 
     def settle(key, number, ref):
         rs_copy(key, number, ref, ref, other_core).wait()
@@ -590,7 +591,7 @@
         with scope("rs_sums"):
             me = place[axes(key)[0]]
             got = r.RA[key]
-            settle(key, 1, got.at[0:2])
+            rs_copy(key, 1, got.at[0:2], got.at[0:2], other_core).wait_recv()
             for way, sign in ((0, 1), (1, -1)):
                 own = r.RC[key][cut(key, wrap(me + sign, 4), 1 - way)]
                 r.CA[key][way] = own + got[3 * way]
@@ -600,7 +601,8 @@
         with scope("rs_second"):
             first, axis, _, at = axes(key)
             got = r.RA[key]
-            settle(key, 2, got.at[0:4])
+            rs_copy(key, 2, got.at[0:4], got.at[0:4], other_core).wait_recv()
+            rs_copy(key, 2, got, got, other_core).wait_send()
             for half in range(2):
                 near, summed = (1, 5) if half == 0 else (4, 2)
                 total = r.RC[key][cut(key, place[first], half)].astype(F32)

time: 62.1 us -> 62 us (level)
  no operation moved by 1% of the time
where the time goes in v4:
time: 62 us; the launch traced here: 61.9 us
  Pallas kernels  60.6 us (98%)
  between operations  1.29 us (2%)
    pallas_call x1, Pallas kernels, body(): pl.pallas_call(kernel, out_shape=jax.ShapeDtypeStruct((SUMS_AT + 72, D),...  58.6 us
    pallas_call x1, Pallas kernels, body(): pl.pallas_call(finish_kernel, out_shape=tuple((jax.ShapeDtypeStruct(shape...  1.97 us

profile of v4, /device:TPU:0, one launch (start us, length us, event | category | flops | bytes accessed | tf_op | source)
XLA Modules:
  0.0 61.9 jit_solution(7531366828452906817)
XLA Ops:
  1.3 58.6 %shard_map.188.sums = f32[328,512]{1,0:T(8,128)} custom-call(bf16[128,512]{1,0:T(8,128)(2,1)} %bitcast.11, bf16[1024,512]{1,0:T(8,128)(2,1)} %bitcast.8, bf16[2,1536,512]{2,1,0:T(8,128)(2,1)} %refs_2_.1, bf16[2,512,512]{2,1,0:T(8,128)(2,1)} %refs_3_.1, bf16[2,1024,512]{2,1,0:T(8,128)(2,1)} %refs_4_.1, bf16[2,512,512]{2,1,0:T(8,128)(2,1)} %refs_5_.1, ...), custom_call_target="tpu_custom_call" | custom-call | flops 10000000000 | bytes 10000000 | tf_op jit(solution)/shard_map/pallas_call | solution.py:746
  59.9 2.0 %shard_map.189 = (f32[128,512]{1,0:T(8,128)}, f32[128,512]{1,0:T(8,128)}, f32[12,2,512]{2,1,0:T(2,128)}, f32[2,4,512]{2,1,0:T(4,128)}, f32[2,8,512]{2,1,0:T(8,12...) custom-call(f32[328,512]{1,0:T(8,128)} %shard_map.188.sums), custom_call_target="tpu_custom_call" | custom-call | tf_op jit(solution)/shard_map/pallas_call | solution.py:780
